TPU v7x, 128 devices: a whole 4x4x4 slice. The times are simulated.
128 devices in a mesh: dp: 16 (over z, x), mp: 8 (over y, core).
Axes of the slice: x: 4, y: 4, z: 4, core: 2. Of those that a mesh axis runs over, the one named last changes fastest.
Arguments:
- gradients: bfloat16 [8, 3584, 14336], P(None, 'dp', 'mp'), may hold values from -60 to 60
- column_slot: int32 [8, 16], replicated, may hold values from 0 to 15, as said below
- left_roots: bfloat16 [16, 8, 4, 896, 896], P('dp', 'mp'), may hold values from -1 to 5
- right_roots: bfloat16 [16, 8, 4, 896, 896], P('dp', 'mp'), may hold values from -1 to 5
Outputs:
- update: bfloat16 [8, 3584, 14336], P(None, 'dp', 'mp')
- clip_scale: float32 [], replicated
Inputs may be any that keep to these rules, and one draw needn't show every extreme that they name: `column_slot`: block column c belongs to group c // 2; over all matrices, the entries of one group's block columns are a permutation of 0 to 15.
All inputs are finite; a program needn't handle non-finite values.
Results may differ from a plain program's by a relative error of at most 0.0049.
Values may be sent and summed in bfloat16 or wider, within the bound.
A program may use at most 128 MiB of HBM per device.

v0:
```python
import functools

import jax
import jax.numpy as jnp
from jax import lax
from jax.sharding import Mesh
from jax.sharding import PartitionSpec as P

D = 3584
FF = 14336
BLOCK = 896
MATRICES = 8
MP = ("mp_0", "mp_1")
DP = ("dp_0", "dp_1")
DP_MP = ("dp_0", "dp_1", "mp_0", "mp_1")


rms_limit = 0.25
epsilon = 1e-06


def over_axes(x, axes):
    return functools.reduce(lax.psum, axes, x)


def split_up(x, dim, devices):
    before, after = (x.shape[:dim], x.shape[dim + 1 :])
    return jnp.moveaxis(x.reshape(*before, devices, -1, *after), dim, 0)


def edges_of(length, count):
    step = length // count
    if step >= 8:
        step -= step % 8
    return [step * k for k in range(1, count)]


def in_order(pieces, dim):
    pieces = jnp.moveaxis(pieces, 0, dim)
    dims = pieces.shape
    return pieces.reshape(*dims[:dim], dims[dim] * dims[dim + 1], *dims[dim + 2 :])


def exchange_in_pieces(x, axis, pieces, split_dim, concat_dim):
    blocks = split_up(x, split_dim, lax.axis_size(axis))
    widest = max(range(1, max(2, blocks.ndim - 1)), key=lambda d: blocks.shape[d])
    gathered = []
    for piece in jnp.split(blocks, edges_of(blocks.shape[widest], pieces), axis=widest):
        if piece.size:
            gathered.append(lax.all_to_all(piece, axis, split_axis=0, concat_axis=0, tiled=True))
    return in_order(jnp.concatenate(gathered, axis=widest), concat_dim)


def body(gradients, column_slot, left_roots, right_roots):
    row_count = gradients.shape[1]
    local_cols = gradients.shape[2] // BLOCK
    slot_count = MATRICES * local_cols
    mp_index = lax.axis_index(MP)
    my_slots = lax.dynamic_slice_in_dim(column_slot, mp_index * local_cols, local_cols, 1).reshape(
        slot_count
    )
    columns = (
        gradients.reshape(MATRICES, row_count, local_cols, BLOCK)
        .transpose(0, 2, 1, 3)
        .reshape(slot_count, row_count, BLOCK)
    )
    send_order = jnp.argsort(my_slots)
    ordered = jnp.take(columns, send_order, axis=0)
    owned_cols = lax.all_to_all(ordered, DP, split_axis=0, concat_axis=1, tiled=True)
    square_sum = over_axes(jnp.sum(jnp.square(owned_cols.astype(jnp.float32))), DP_MP)
    clip_scale = jnp.minimum(
        jnp.float32(1.0), rms_limit / jnp.sqrt(square_sum / (MATRICES * D * FF) + epsilon)
    )
    owned_count = owned_cols.shape[0]
    owned_blocks = owned_cols.reshape(owned_count, D // BLOCK, BLOCK, BLOCK)
    left_root = left_roots[:, 0]
    right_root = right_roots[:, 0]
    first_product = jnp.einsum(
        "snab,snbc->snac", left_root, owned_blocks, preferred_element_type=jnp.float32
    )
    scaled = (clip_scale * first_product).astype(jnp.bfloat16)
    second_product = jnp.einsum(
        "snab,snbc->snac", scaled, right_root, preferred_element_type=jnp.float32
    )
    finished = second_product.astype(jnp.bfloat16).reshape(owned_count, D, BLOCK)
    returned = exchange_in_pieces(finished, DP, 2, 1, 0)
    restored = jnp.take(returned, my_slots, axis=0)
    update = (
        restored.reshape(MATRICES, local_cols, row_count, BLOCK)
        .transpose(0, 2, 1, 3)
        .reshape(MATRICES, row_count, local_cols * BLOCK)
    )
    return (update, clip_scale)


def solution(mesh):
    finer = Mesh(mesh.devices.reshape(4, 4, 4, 2), ("dp_0", "dp_1", "mp_0", "mp_1"))
    return jax.shard_map(
        body,
        mesh=finer,
        in_specs=(P(None, DP, MP), P(), P(DP, MP, None, None, None), P(DP, MP, None, None, None)),
        out_specs=(P(None, DP, MP), P()),
        check_vma=False,
    )
```

profile of v0, /device:TPU:0, one launch (start us, length us, event | category | flops | bytes accessed | tf_op | source)
XLA Modules:
  0.0 284.6 jit_solution(10779204279375044281)
XLA Ops:
  0.6 0.0 copy-start
  0.7 0.7 copy-done
  1.3 0.1 constant_dynamic-slice_fusion
  1.4 0.1 reshape.55
  1.5 1.3 sort.17
  2.8 3.4 %fusion.11 = (bf16[8,224,896]{2,1,0:T(8,128)(2,1)S(1)}, bf16[8,224,896]{2,1,0:T(8,128)(2,1)S(1)}) fusion(bf16[8,224,1792]{2,1,0:T(8,128)(2,1)} %param.6), kind=kLoop, calls=%fused_computation.21 | loop fusion | bytes 12845056 | tf_op jit(solution)/shard_map/slice
  6.2 3.6 %pad_maximum_fusion = bf16[8,448,896]{2,1,0:T(8,128)(2,1)} fusion(bf16[8,224,896]{2,1,0:T(8,128)(2,1)S(1)} %get-tuple-element.8, bf16[8,224,896]{2,1,0:T(8,128)(2,1)S(1)} %get-tuple-element.7), kind=kLoop, calls=%fused_computation.4 | loop fusion | flops 12845056 | bytes 12845056 | tf_op jit(solution)/shard_map/concatenate
  9.8 6.8 %gather_fusion = bf16[16,224,896]{2,1,0:T(8,128)(2,1)} fusion(bf16[16,224,896]{2,1,0:T(8,128)(2,1)} %bitcast.26, s32[1024]{0:T(1024)S(1)} %pad_clamp_fusion.1), kind=kCustom, calls=%fused_computation.clone | custom fusion | bytes 12845120 | tf_op jit(solution)/shard_map/jit(_take)/gather | solution.py:68
  16.6 3.5 %broadcast_select_fusion.1 = bf16[16,224,896]{2,1,0:T(8,128)(2,1)S(1)} fusion(bf16[16,224,896]{2,1,0:T(8,128)(2,1)} %gather_fusion, pred[16]{0:T(512)(128)(4,1)S(1)} %compare_and_fusion.1), kind=kLoop, calls=%fused_computation.11 | loop fusion | flops 3211264 | bytes 12845072 | tf_op jit(solution)/shard_map/jit(_take)/select_n | solution.py:68
  20.1 82.5 %all_to_all.19 = bf16[16,224,896]{2,1,0:T(8,128)(2,1)S(1)} all-to-all(bf16[16,224,896]{2,1,0:T(8,128)(2,1)S(1)} %broadcast_select_fusion.1), channel_id=1, replica_groups=mesh['dp_0'=4,'dp_1'=4,'mp_0'=4,'mp_1'=2] {'dp_0','dp_1'}, dimensions={0} | all-to-all | bytes 12845056 | tf_op jit(solution)/shard_map/all_to_all | solution.py:69
  102.6 0.0 copy-start.2
  102.6 2.7 copy-done.2
  105.4 3.9 %multiply_reduce_fusion = f32[]{:T(128)} fusion(bf16[16,224,896]{2,1,0:T(8,128)(2,1)S(1)} %all_to_all.19), kind=kLoop, calls=%fused_computation.3 | loop fusion | flops 9633791 | bytes 6422532 | tf_op jit(solution)/shard_map/reduce_sum | solution.py:70
  109.3 9.2 %psum.28 = f32[]{:T(128)} all-reduce(f32[]{:T(128)} %multiply_reduce_fusion), channel_id=1, replica_groups=mesh['dp_0'=4,'dp_1'=4,'mp_0'=4,'mp_1'=2] {'dp_0'}, use_global_device_ids=true, to_apply=%region_2.4 | all-reduce | flops 1 | bytes 8 | tf_op jit(solution)/shard_map/psum | solution.py:23
  118.5 9.6 %psum.29 = f32[]{:T(128)} all-reduce(f32[]{:T(128)} %psum.28), channel_id=1, replica_groups=mesh['dp_0'=4,'dp_1'=4,'mp_0'=4,'mp_1'=2] {'dp_1'}, use_global_device_ids=true, to_apply=%region_3.5 | all-reduce | flops 1 | bytes 8 | tf_op jit(solution)/shard_map/psum | solution.py:23
  128.0 11.4 %psum.30 = f32[]{:T(128)} all-reduce(f32[]{:T(128)} %psum.29), channel_id=1, replica_groups=mesh['dp_0'=4,'dp_1'=4,'mp_0'=4,'mp_1'=2] {'mp_0'}, use_global_device_ids=true, to_apply=%region_4.6 | all-reduce | flops 1 | bytes 8 | tf_op jit(solution)/shard_map/psum | solution.py:23
  139.4 3.1 %psum.31 = f32[]{:T(128)} all-reduce(f32[]{:T(128)} %psum.30), channel_id=1, replica_groups=mesh['dp_0'=4,'dp_1'=4,'mp_0'=4,'mp_1'=2] {'mp_1'}, use_global_device_ids=true, to_apply=%region_5.7 | all-reduce | flops 1 | bytes 8 | tf_op jit(solution)/shard_map/psum | solution.py:23
  143.2 20.6 %fusion.5 = bf16[4,896,896]{2,1,0:T(8,128)(2,1)} fusion(bf16[1,1,4,896,896]{4,3,2,1,0:T(8,128)(2,1)} %param.9, bf16[4,896,896]{2,1,0:T(8,128)(2,1)} %bitcast.25, bf16[1,1,4,896,896]{4,3,2,1,0:T(8,128)(2,1)} %param.8, f32[]{:T(128)} %min_shard_map.3), kind=kOutput, calls=%fused_computation.12 | convolution fusion | flops 11518803968 | bytes 25690116 | tf_op jit(solution)/shard_map/snab,snbc->snac/dot_general | solution.py:82
  163.8 5.1 %fusion.10 = (bf16[16,1,112,896]{3,2,1,0:T(8,128)(2,1)S(1)}, bf16[16,1,112,896]{3,2,1,0:T(8,128)(2,1)}) fusion(bf16[16,1,224,896]{3,2,1,0:T(8,128)(2,1)} %bitcast.29), kind=kLoop, calls=%fused_computation.20 | loop fusion | bytes 12845056 | tf_op jit(solution)/shard_map/split | solution.py:48
  168.8 43.8 %all_to_all.20 = bf16[16,1,112,896]{3,2,1,0:T(8,128)(2,1)S(1)} all-to-all(bf16[16,1,112,896]{3,2,1,0:T(8,128)(2,1)S(1)} %get-tuple-element.5), channel_id=1, replica_groups=mesh['dp_0'=4,'dp_1'=4,'mp_0'=4,'mp_1'=2] {'dp_0','dp_1'}, dimensions={0} | all-to-all | bytes 6422528 | tf_op jit(solution)/shard_map/all_to_all | solution.py:50
  212.6 4.7 %all-to-all-start.2 = ((bf16[16,1,112,896]{3,2,1,0:T(8,128)(2,1)}), bf16[16,1,112,896]{3,2,1,0:T(8,128)(2,1)}, u32[]{:S(2)}, u32[]{:S(2)}) async-start(bf16[16,1,112,896]{3,2,1,0:T(8,128)(2,1)} %get-tuple-element.6), calls=%async_computation.2 | async-start | bytes 6422528 | tf_op jit(solution)/shard_map/all_to_all | solution.py:50
  217.3 47.4 %all-to-all-done.2 = bf16[16,1,112,896]{3,2,1,0:T(8,128)(2,1)} async-done(((bf16[16,1,112,896]{3,2,1,0:T(8,128)(2,1)}), bf16[16,1,112,896]{3,2,1,0:T(8,128)(2,1)}, u32[]{:S(2)}, u32[]{:S(2)}) %all-to-all-start.2) | async-done | bytes 3211296 | tf_op jit(solution)/shard_map/all_to_all | solution.py:50
  264.7 5.2 %maximum_bitcast_fusion = bf16[16,224,896]{2,1,0:T(8,128)(2,1)} fusion(bf16[16,1,112,896]{3,2,1,0:T(8,128)(2,1)} %all-to-all-done.2, bf16[16,1,112,896]{3,2,1,0:T(8,128)(2,1)S(1)} %all_to_all.20), kind=kLoop, calls=%fused_computation.5 | loop fusion | flops 12845056 | bytes 12845056 | tf_op jit(solution)/shard_map/reshape | solution.py:41
  269.9 6.8 %gather_fusion.1 = bf16[16,224,896]{2,1,0:T(8,128)(2,1)} fusion(bf16[16,224,896]{2,1,0:T(8,128)(2,1)} %maximum_bitcast_fusion, s32[1024]{0:T(1024)S(1)} %pad_clamp_fusion), kind=kCustom, calls=%fused_computation.1.clone | custom fusion | bytes 12845120 | tf_op jit(solution)/shard_map/jit(_take)/gather | solution.py:87
  276.7 3.5 %broadcast_select_fusion = bf16[16,224,896]{2,1,0:T(8,128)(2,1)S(1)} fusion(bf16[16,224,896]{2,1,0:T(8,128)(2,1)} %gather_fusion.1, pred[16]{0:T(512)(128)(4,1)S(1)} %compare_and_fusion), kind=kLoop, calls=%fused_computation.10 | loop fusion | flops 3211264 | bytes 12845072 | tf_op jit(solution)/shard_map/jit(_take)/select_n | solution.py:87
  280.2 0.0 copy-start.1
  280.2 3.3 %copy.10 = bf16[8,2,28,8,896]{4,3,1,2,0:T(8,128)(2,1)} copy(bf16[8,2,28,8,896]{4,3,2,1,0:T(8,128)(2,1)S(1)} %bitcast.27) | data formatting | bytes 12845056 | tf_op jit(solution)/shard_map/reshape | solution.py:91
  283.5 0.0 copy-done.1
  (7 shorter events, 0.0 us)
Async XLA Ops:
  0.6 0.7 copy-start
  102.6 2.7 copy-start.2
  212.6 52.1 %all-to-all-start.2 = ((bf16[16,1,112,896]{3,2,1,0:T(8,128)(2,1)}), bf16[16,1,112,896]{3,2,1,0:T(8,128)(2,1)}, u32[]{:S(2)}, u32[]{:S(2)}) async-start(bf16[16,1,112,896]{3,2,1,0:T(8,128)(2,1)} %get-tuple-element.6), calls=%async_computation.2 | async-start | bytes 6422528 | tf_op jit(solution)/shard_map/all_to_all | solution.py:50
  280.2 3.3 %copy-start.1 = (s32[8,16]{1,0:T(8,128)S(1)}, s32[8,16]{1,0:T(8,128)}, u32[]{:S(2)}) copy-start(s32[8,16]{1,0:T(8,128)} %param.7) | copy-start | bytes 1540
where the time goes:
time: 285 us
  blocking collectives  159 us (56%)
  waiting for transfers between devices  47.4 us (17%)
  local copies, waits for them, and re-layouts  28.9 us (10%)
  other arithmetic  21 us (7%)
  matrix products  20.6 us (7%)
  starting transfers between devices  4.66 us (2%)
    all_to_all x1, blocking collectives, body(): lax.all_to_all(ordered, DP, split_axis=0, concat_axis=1, tiled=True)  82.5 us
    all_to_all x1, waiting for transfers between devices, exchange_in_pieces(): lax.all_to_all(piece, axis, split_axis=0, concat_axis=0, tiled=True)  47.4 us
    all_to_all x1, blocking collectives, exchange_in_pieces(): lax.all_to_all(piece, axis, split_axis=0, concat_axis=0, tiled=True)  43.8 us
    psum x4, blocking collectives, over_axes(): return functools.reduce(lax.psum, axes, x)  33.2 us
    dot_general x1, matrix products, body(): jnp.einsum('snab,snbc->snac', scaled, right_root, preferred_element_type=...  20.6 us
    gather x1, local copies, waits for them, and re-layouts, body(): restored = jnp.take(returned, my_slots, axis=0)  6.8 us
    gather x1, local copies, waits for them, and re-layouts, body(): ordered = jnp.take(columns, send_order, axis=0)  6.8 us
  transfers between devices with their start and end apart: 1, of which 1 were waited for; matrix products, arithmetic and copies ran while one was open for 0% of the time, Pallas kernels for 0%

commit v1 on v0

v1 whole, which is shorter than its diff:
```python
import functools

import jax
import jax.numpy as jnp
from jax import lax
from jax.experimental import pallas as pl
from jax.experimental.pallas import tpu as pltpu
from jax.sharding import PartitionSpec as P

D = 3584
FF = 14336
BLOCK = 896
MATRICES = 8
ROW_BLOCKS = 4
ROWS = 224
N_DP = 16
N_MP = 8
COLS = 2
SLOTS = 16
PART = 32
PARTS = ROWS // PART
LIMIT = 0.25
EPSILON = 1e-6
MESH = pl.DeviceIdType.MESH


def offset(dz, dx):
    return (dz % 4) * 4 + dx % 4


NEAR = [offset(*o) for o in ((1, 0), (3, 0), (1, 1), (3, 3), (1, 3), (3, 1), (1, 2), (3, 2))]
REST = [offset(*o) for o in ((0, 1), (0, 3), (2, 0), (2, 1), (2, 3), (0, 2), (2, 2))]


def exchange_kernel(
    slot, gradients, left, right, ret, clip_out,
    own, send, recv, lbuf, rbuf, inverse, acc, mp_sums, dp_sums,
    own_sem, root_sem, fwd_send, fwd_recv, ret_send, ret_recv, mp_send, mp_recv, dp_send, dp_recv,
):
    me = lax.axis_index("dp")
    mp = lax.axis_index("mp")
    z, x = me // 4, me % 4

    def device(k):
        return lax.rem(z + k // 4, 4) * 4 + lax.rem(x + k % 4, 4)

    loads = []
    for c in range(COLS):
        for m in range(MATRICES):
            copy = pltpu.make_async_copy(
                gradients.at[m, :, pl.ds(c * BLOCK, BLOCK)], own.at[c * MATRICES + m], own_sem.at[c * MATRICES + m]
            )
            copy.start()
            loads.append(copy)

    barrier = pltpu.get_barrier_semaphore()
    for k in range(1, N_DP):
        pl.semaphore_signal(barrier, inc=1, device_id={"dp": device(k)}, device_id_type=MESH)
    for k in range(1, N_MP):
        pl.semaphore_signal(barrier, inc=1, device_id={"mp": lax.rem(mp + k, N_MP)}, device_id_type=MESH)

    slots = [slot[m, mp * COLS + c] for c in range(COLS) for m in range(MATRICES)]
    for k in range(N_DP):
        target = device(k)
        found = jnp.int32(0)
        for j, value in enumerate(slots):
            found = jnp.where(value == target, jnp.int32(j), found)
        inverse[k] = found

    for copy in loads:
        copy.wait()
    roots = []
    for r in range(ROW_BLOCKS):
        for h, (src, dst) in enumerate(((left, lbuf), (right, rbuf))):
            copy = pltpu.make_async_copy(src.at[0, 0, r], dst.at[r], root_sem.at[2 * r + h])
            copy.start()
            roots.append(copy)

    acc[...] = jnp.zeros_like(acc)

    def stage(p):
        rows = pl.ds(p * PART, PART)
        total = acc[...]
        for k in range(N_DP):
            block = own[inverse[k], rows, :]
            if k == 0:
                recv[z, pl.ds(x * ROWS + p * PART, PART), :] = block
            else:
                send[k, rows, :] = block
            wide = block.astype(jnp.float32)
            square = wide * wide
            for lane in range(0, BLOCK, 128):
                total = total + square[:, lane : lane + 128]
        acc[...] = total

    def send_part(k, p):
        rows = pl.ds(p * PART, PART)
        pltpu.make_async_remote_copy(
            src_ref=send.at[k, rows],
            dst_ref=recv.at[z, pl.ds(x * ROWS + p * PART, PART)],
            send_sem=fwd_send.at[k],
            recv_sem=fwd_recv.at[k // 4],
            device_id={"dp": device(k)},
            device_id_type=MESH,
        ).start()

    def send_parts(offsets, first, last):
        @pl.loop(first, last)
        def _(p):
            for k in offsets:
                send_part(k, p)

    stage(0)
    stage(1)
    pl.semaphore_wait(barrier, N_DP + N_MP - 2)
    send_parts(NEAR, 0, 1)

    @pl.loop(2, PARTS)
    def _(p):
        stage(p)

    send_parts(NEAR, 1, 2)

    part = acc[...]
    mp_sums[mp] = part[0:8] + part[8:16] + part[16:24] + part[24:32]
    mp_copies = []
    for k in range(1, N_MP):
        copy = pltpu.make_async_remote_copy(
            src_ref=mp_sums.at[mp],
            dst_ref=mp_sums.at[mp],
            send_sem=mp_send.at[k],
            recv_sem=mp_recv.at[k],
            device_id={"mp": lax.rem(mp + k, N_MP)},
            device_id_type=MESH,
        )
        copy.start()
        mp_copies.append(copy)
    for copy in mp_copies:
        copy.wait()
    total = mp_sums[0]
    for i in range(1, N_MP):
        total = total + mp_sums[i]
    dp_sums[me] = total
    dp_copies = []
    for k in range(1, N_DP):
        copy = pltpu.make_async_remote_copy(
            src_ref=dp_sums.at[me],
            dst_ref=dp_sums.at[me],
            send_sem=dp_send.at[k],
            recv_sem=dp_recv.at[k],
            device_id={"dp": device(k)},
            device_id_type=MESH,
        )
        copy.start()
        dp_copies.append(copy)

    send_parts(NEAR, 2, PARTS)
    send_parts(REST, 0, PARTS)

    for copy in dp_copies:
        copy.wait()
    total = dp_sums[0]
    for i in range(1, N_DP):
        total = total + dp_sums[i]
    square_sum = jnp.broadcast_to(jnp.sum(total, keepdims=True), (8, 128))
    clip = jnp.minimum(jnp.float32(1.0), LIMIT / jnp.sqrt(square_sum / (MATRICES * D * FF) + EPSILON))
    clip_out[...] = clip
    scale = jnp.broadcast_to(clip[0:1, 0:1], (1, BLOCK))

    for copy in roots:
        copy.wait()

    def wait_block(dz):
        rows = BLOCK if dz else BLOCK - ROWS
        pltpu.make_async_copy(
            recv.at[0, pl.ds(0, rows)], recv.at[0, pl.ds(0, rows)], fwd_recv.at[dz]
        ).wait()

    def compute(dz):
        wait_block(dz)
        r = lax.rem(z + 4 - dz, 4)

        @pl.loop(0, 4)
        def _(i):
            product = jnp.dot(lbuf[r, pl.ds(i * ROWS, ROWS), :], recv[r], preferred_element_type=jnp.float32)
            scaled = (scale * product).astype(jnp.bfloat16)
            second = jnp.dot(scaled, rbuf[r], preferred_element_type=jnp.float32)
            own[r * 4 + i] = second.astype(jnp.bfloat16)

    def return_part(k, p):
        rows = pl.ds(p * PART, PART)
        pltpu.make_async_remote_copy(
            src_ref=own.at[device(k), rows],
            dst_ref=ret.at[me, rows],
            send_sem=ret_send.at[k],
            recv_sem=ret_recv.at[k],
            device_id={"dp": device(k)},
            device_id_type=MESH,
        ).start()

    def return_parts(offsets):
        @pl.loop(0, PARTS)
        def _(p):
            for k in offsets:
                return_part(k, p)

    compute(1)
    compute(3)
    return_parts(NEAR)
    compute(2)
    compute(0)
    return_parts(REST)
    ret[me] = own[me]

    for k in range(1, N_DP):
        for sem in (fwd_send, ret_send, ret_recv):
            pltpu.make_async_copy(send.at[k], send.at[k], sem.at[k]).wait()


def place_kernel(slot, ret, update, sem):
    mp = lax.axis_index("mp")
    copies = []
    for c in range(COLS):
        for m in range(MATRICES):
            copy = pltpu.make_async_copy(
                ret.at[slot[m, mp * COLS + c]], update.at[m, :, pl.ds(c * BLOCK, BLOCK)], sem.at[c * MATRICES + m]
            )
            copy.start()
            copies.append(copy)
    for copy in copies:
        copy.wait()


def body(gradients, column_slot, left_roots, right_roots):
    block = (ROW_BLOCKS, BLOCK, BLOCK)
    columns = (SLOTS, ROWS, BLOCK)
    bf16, f32 = jnp.bfloat16, jnp.float32
    dma = pltpu.SemaphoreType.DMA
    anywhere = pl.BlockSpec(memory_space=pl.ANY)
    vmem = pl.BlockSpec(memory_space=pltpu.VMEM)
    smem = pl.BlockSpec(memory_space=pltpu.SMEM)
    ret, clip = pl.pallas_call(
        exchange_kernel,
        out_shape=(jax.ShapeDtypeStruct(columns, bf16), jax.ShapeDtypeStruct((8, 128), f32)),
        in_specs=[smem, anywhere, anywhere, anywhere],
        out_specs=(vmem, vmem),
        scratch_shapes=[
            pltpu.VMEM(columns, bf16),
            pltpu.VMEM(columns, bf16),
            pltpu.VMEM(block, bf16),
            pltpu.VMEM(block, bf16),
            pltpu.VMEM(block, bf16),
            pltpu.SMEM((N_DP,), jnp.int32),
            pltpu.VMEM((PART, 128), f32),
            pltpu.VMEM((N_MP, 8, 128), f32),
            pltpu.VMEM((N_DP, 8, 128), f32),
            dma((COLS * MATRICES,)),
            dma((2 * ROW_BLOCKS,)),
            dma((N_DP,)),
            dma((4,)),
            dma((N_DP,)),
            dma((N_DP,)),
            dma((N_MP,)),
            dma((N_MP,)),
            dma((N_DP,)),
            dma((N_DP,)),
        ],
        compiler_params=pltpu.CompilerParams(
            collective_id=0, has_side_effects=True, vmem_limit_bytes=54 * 2**20
        ),
        name="exchange",
    )(column_slot, gradients, left_roots, right_roots)
    update = pl.pallas_call(
        place_kernel,
        out_shape=jax.ShapeDtypeStruct((MATRICES, ROWS, COLS * BLOCK), bf16),
        in_specs=[smem, vmem],
        out_specs=anywhere,
        scratch_shapes=[dma((COLS * MATRICES,))],
        compiler_params=pltpu.CompilerParams(vmem_limit_bytes=12 * 2**20),
        name="place",
    )(column_slot, ret)
    return update, clip[0, 0]


def solution(mesh):
    return jax.shard_map(
        body,
        mesh=mesh,
        in_specs=(P(None, "dp", "mp"), P(), P("dp", "mp"), P("dp", "mp")),
        out_specs=(P(None, "dp", "mp"), P()),
        check_vma=False,
    )
```

time: 285 us -> 169 us (0.59)
  Pallas kernels: 0 us -> 164 us
  blocking collectives: 159 us -> 0 us
  waiting for transfers between devices: 47.4 us -> 0 us
  local copies, waits for them, and re-layouts: 28.9 us -> 4.02 us
  other arithmetic: 21 us -> 0 us
  matrix products: 20.6 us -> 0 us
  starting transfers between devices: 4.66 us -> 0 us
    pallas_call x0 -> x2, Pallas kernels: none -> 164 us  [the longest x1 161 us: body(): pl.pallas_call(exchange_kernel, out_shape=(jax.ShapeDtypeStruct(columns,...]
    all_to_all x2 -> x0, blocking collectives: 126 us -> none  [the longest x1 82.5 us: body(): lax.all_to_all(ordered, DP, split_axis=0, concat_axis=1, tiled=True)]
    all_to_all x1 -> x0, waiting for transfers between devices: 47.4 us -> none  [exchange_in_pieces(): lax.all_to_all(piece, axis, split_axis=0, concat_axis=0, tiled=True)]
    psum x4 -> x0, blocking collectives: 33.2 us -> none  [over_axes(): return functools.reduce(lax.psum, axes, x)]
    dot_general x1 -> x0, matrix products: 20.6 us -> none  [body(): jnp.einsum('snab,snbc->snac', scaled, right_root, preferred_element_type=...]
    gather x2 -> x0, local copies, waits for them, and re-layouts: 13.6 us -> none  [the longest x1 6.8 us: body(): restored = jnp.take(returned, my_slots, axis=0)]
    select_n x4 -> x0, other arithmetic: 7.04 us -> none  [the longest x2 3.52 us: body(): restored = jnp.take(returned, my_slots, axis=0)]
    reshape x1 -> x0, other arithmetic: 5.17 us -> none  [in_order(): pieces.reshape(*dims[:dim], dims[dim] * dims[dim + 1], *dims[dim + 2:])]
  transfers between devices with their start and end apart: 1 -> 0, of which waited for: 1 -> 0; matrix products, arithmetic and copies ran while one was open for 0% -> 0% of each run, Pallas kernels for 0% -> 0%
where the time goes in v1:
time: 169 us
  Pallas kernels  164 us (97%)
  local copies, waits for them, and re-layouts  4.02 us (2%)
    pallas_call x1, Pallas kernels, body(): pl.pallas_call(exchange_kernel, out_shape=(jax.ShapeDtypeStruct(columns,...  161 us
    pallas_call x1, Pallas kernels, body(): pl.pallas_call(place_kernel, out_shape=jax.ShapeDtypeStruct((MATRICES, RO...  3.43 us

profile of v1, /device:TPU:0, one launch (start us, length us, event | category | flops | bytes accessed | tf_op | source)
XLA Modules:
  0.0 168.6 jit_solution(15931938512512313266)
XLA Ops:
  0.6 0.0 copy-start.1
  0.6 160.5 %exchange.1 = (bf16[16,224,896]{2,1,0:T(8,128)(2,1)}, f32[8,128]{1,0:T(8,128)}) custom-call(s32[8,16]{1,0:T(8,128)} %slot.3, bf16[8,224,1792]{2,1,0:T(8,128)(2,1)} %gradients.1, bf16[1,1,4,896,896]{4,3,2,1,0:T(8,128)(2,1)} %left.1, bf16[1,1,4,896,896]{4,3,2,1,0:T(8,128)(2,1)} %right.1), custom_call_target="tpu_custom_call" | custom-call | tf_op jit(solution)/shard_map/exchange/pallas_call | solution.py:242
  161.2 1.2 slice.3
  162.4 0.0 copy-done.1
  162.4 0.0 copy-start
  162.4 2.8 %copy-done = bf16[16,224,896]{2,1,0:T(8,128)(2,1)S(1)} copy-done((bf16[16,224,896]{2,1,0:T(8,128)(2,1)S(1)}, bf16[16,224,896]{2,1,0:T(8,128)(2,1)}, u32[]{:S(2)}) %copy-start) | copy-done | bytes 6422552
  165.2 3.4 %place.1 = bf16[8,224,1792]{2,1,0:T(8,128)(2,1)} custom-call(s32[8,16]{1,0:T(8,128)S(1)} %copy-done.1, bf16[16,224,896]{2,1,0:T(8,128)(2,1)S(1)} %copy-done), custom_call_target="tpu_custom_call" | custom-call | tf_op jit(solution)/shard_map/place/pallas_call | solution.py:273
Async XLA Ops:
  0.6 161.7 %copy-start.1 = (s32[8,16]{1,0:T(8,128)S(1)}, s32[8,16]{1,0:T(8,128)}, u32[]{:S(2)}) copy-start(s32[8,16]{1,0:T(8,128)} %slot.3) | copy-start | bytes 1540
  162.4 2.8 %copy-start = (bf16[16,224,896]{2,1,0:T(8,128)(2,1)S(1)}, bf16[16,224,896]{2,1,0:T(8,128)(2,1)}, u32[]{:S(2)}) copy-start(bf16[16,224,896]{2,1,0:T(8,128)(2,1)} %get-tuple-element.4.ret) | copy-start | bytes 19267588
